TPU v7x, 8 devices: a whole 2x2x1 slice. The times are simulated.
8 devices in a mesh: data: 1 (over z), dap2: 2 (over y), dap: 4 (over x, core).
Axes of the slice: x: 2, y: 2, z: 1, core: 2. Of those that a mesh axis runs over, the one named last changes fastest.
Arguments:
- pair_act: bfloat16 [256, 256, 64], P(('data', 'dap'), 'dap2')
- pair_mask: int32 [256, 256], P(('data', 'dap'), 'dap2')
- in_gamma: float32 [24, 2, 64], replicated
- in_beta: float32 [24, 2, 64], replicated
- w_proj: bfloat16 [24, 2, 64, 256], replicated
- w_gate: bfloat16 [24, 2, 64, 64], replicated
- out_gamma: float32 [24, 2, 64], replicated
- out_beta: float32 [24, 2, 64], replicated
- w_out: bfloat16 [24, 2, 64, 64], replicated
Outputs:
- output: bfloat16 [256, 256, 64], P(('data', 'dap'), 'dap2')
All inputs are finite; a program needn't handle non-finite values.
Results may differ from a plain program's by a relative error of at most 0.02.
Values are sent between devices in bfloat16 or wider.
A program may use at most 1 GiB of HBM per device.

v0:
```python
import jax
import jax.numpy as jnp
from jax import lax
from jax.sharding import PartitionSpec as P

NORM_EPS = 1e-5
OUT_FORM = 'cik,cjk->cij'
IN_FORM = 'cki,ckj->cij'


def layer_norm(values, gamma, beta, axis):
    centered = values - jnp.mean(values, axis=axis, keepdims=True)
    variance = jnp.mean(centered * centered, axis=axis, keepdims=True)
    return centered * lax.rsqrt(variance + NORM_EPS) * gamma + beta


def project_local(pair_blk, mask_f, gamma_in, beta_in, w_proj, w_gate):
    tri_dim = w_proj.shape[1] // 4
    normed = layer_norm(pair_blk.astype(jnp.float32), gamma_in, beta_in, -1).astype(jnp.bfloat16)
    projected = jnp.einsum('ijd,dgc->gcij', normed, w_proj.reshape(w_proj.shape[0], 4, tri_dim), preferred_element_type=jnp.float32)
    left = (mask_f * jax.nn.sigmoid(projected[1]) * projected[0]).astype(jnp.bfloat16)
    right = (mask_f * jax.nn.sigmoid(projected[3]) * projected[2]).astype(jnp.bfloat16)
    gate = jax.nn.sigmoid(jnp.einsum('ijd,de->ije', normed, w_gate, preferred_element_type=jnp.float32))
    return left, right, gate


def finish_local(pair_blk, tri_blk, gate, gamma_out, beta_out, w_out):
    tri_normed = layer_norm(tri_blk.astype(jnp.float32), gamma_out[:, None, None], beta_out[:, None, None], 0).astype(jnp.bfloat16)
    update = jnp.einsum('cij,cd->ijd', tri_normed, w_out, preferred_element_type=jnp.float32)
    return (pair_blk.astype(jnp.float32) + gate * update).astype(jnp.bfloat16)


def to_channels(block):
    col_full = lax.all_to_all(block, 'dap2', 0, 2, tiled=True)
    return lax.all_to_all(col_full, 'dap', 0, 1, tiled=True)


def from_channels(block):
    row_part = lax.all_to_all(block, 'dap', 1, 0, tiled=True)
    return lax.all_to_all(row_part, 'dap2', 2, 0, tiled=True)


def triangle_update(pair_blk, mask_f, params, einsum_form):
    gamma_in, beta_in, w_proj, w_gate, gamma_out, beta_out, w_out = params
    left, right, gate = project_local(pair_blk, mask_f, gamma_in, beta_in, w_proj, w_gate)
    left_ch = to_channels(left)
    right_ch = to_channels(right)
    tri_ch = jnp.einsum(einsum_form, left_ch, right_ch, preferred_element_type=jnp.float32).astype(jnp.bfloat16)
    return finish_local(pair_blk, from_channels(tri_ch), gate, gamma_out, beta_out, w_out)


def solution(mesh):
    pair_spec = P(('data', 'dap'), 'dap2', None)
    mask_spec = P(('data', 'dap'), 'dap2')
    weight_spec = P()

    def local_fn(pair_act, pair_mask, in_gamma, in_beta, w_proj, w_gate, out_gamma, out_beta, w_out):
        mask_f = pair_mask.astype(jnp.float32)
        weights = (in_gamma, in_beta, w_proj, w_gate, out_gamma, out_beta, w_out)
        for layer in range(in_gamma.shape[0]):
            for direction, einsum_form in enumerate((OUT_FORM, IN_FORM)):
                params = tuple(leaf[layer, direction] for leaf in weights)
                pair_act = triangle_update(pair_act, mask_f, params, einsum_form)
        return pair_act

    return jax.shard_map(local_fn, mesh=mesh, in_specs=(pair_spec, mask_spec) + (weight_spec,) * 7, out_specs=pair_spec, check_vma=False)
```

profile of v0, /device:TPU:0, one launch (start us, length us, event | category | flops | bytes accessed | tf_op | source)
XLA Modules:
  0.0 6180.1 jit_solution(3877531464445553961)
XLA Ops:
  85.5 17.1 all_to_all.4752
  216.2 16.9 all_to_all.4753
  342.6 16.9 all_to_all.4754
  456.8 14.1 all-to-all-done.21
  473.3 16.9 all_to_all.4755
  599.8 16.9 all_to_all.4756
  730.4 16.9 all_to_all.4757
  857.0 16.9 all_to_all.4758
  987.7 16.9 all_to_all.4759
  1114.1 16.9 all_to_all.4760
  1357.1 14.1 all-to-all-done.63
  1373.5 16.9 all_to_all.4761
  1499.9 16.9 all_to_all.4762
  1626.4 16.9 all_to_all.4763
  1757.1 16.9 all_to_all.4764
  1883.5 16.9 all_to_all.4765
  2014.2 16.9 all_to_all.4766
  2140.8 16.9 all_to_all.4767
  2271.3 16.9 all_to_all.4768
  2397.8 16.9 all_to_all.4769
  2528.6 16.9 all_to_all.4770
  2655.0 16.9 all_to_all.4771
  2785.7 16.9 all_to_all.4772
  2912.4 16.9 all_to_all.4773
  3042.9 16.9 all_to_all.4774
  3169.5 16.9 all_to_all.4775
  3300.2 16.9 all_to_all.4776
  3426.6 16.9 all_to_all.4777
  3686.1 16.9 all_to_all.4778
  3812.4 16.9 all_to_all.4779
  3943.1 16.9 all_to_all.4780
  4069.7 16.9 all_to_all.4781
  4200.1 16.9 all_to_all.4782
  4326.6 16.9 all_to_all.4783
  4457.3 16.9 all_to_all.4784
  4583.7 16.9 all_to_all.4785
  4714.4 16.9 all_to_all.4786
  4841.0 16.9 all_to_all.4787
  4971.5 16.9 all_to_all.4788
  5098.1 16.9 all_to_all.4789
  5228.9 16.9 all_to_all.4790
  5355.3 16.9 all_to_all.4791
  5486.0 16.9 all_to_all.4792
  5612.6 16.9 all_to_all.4793
  5743.1 16.9 all_to_all.4794
  5869.7 16.9 all_to_all.4795
  5996.4 16.9 all_to_all.4796
  6126.9 16.9 all_to_all.4797
  (2663 shorter events, 5363.1 us)
Async XLA Ops:
  11.5 18.9 all-to-all-start
  64.7 18.4 all-to-all-start.3
  195.4 18.4 all-to-all-start.9
  321.8 18.4 all-to-all-start.15
  452.5 18.4 all-to-all-start.21
  579.1 18.4 all-to-all-start.27
  709.6 18.4 all-to-all-start.33
  836.2 18.4 all-to-all-start.39
  966.9 18.4 all-to-all-start.45
  1093.3 18.4 all-to-all-start.51
  1219.9 18.4 all-to-all-start.57
  1352.8 18.4 all-to-all-start.63
  1479.1 18.4 all-to-all-start.69
  1605.6 18.4 all-to-all-start.75
  1736.3 18.4 all-to-all-start.81
  1862.7 18.4 all-to-all-start.87
  1993.4 18.4 all-to-all-start.93
  2120.0 18.4 all-to-all-start.99
  2250.5 18.4 all-to-all-start.105
  2377.1 18.4 all-to-all-start.111
  2507.8 18.4 all-to-all-start.117
  2634.2 18.4 all-to-all-start.123
  2764.9 18.4 all-to-all-start.129
  2891.6 18.4 all-to-all-start.135
  3022.1 18.4 all-to-all-start.141
  3148.7 18.4 all-to-all-start.147
  3279.4 18.4 all-to-all-start.153
  3405.9 18.4 all-to-all-start.159
  3532.4 18.4 all-to-all-start.165
  3665.3 18.4 all-to-all-start.171
  3791.6 18.4 all-to-all-start.177
  3922.3 18.4 all-to-all-start.183
  4048.9 18.4 all-to-all-start.189
  4179.3 18.4 all-to-all-start.195
  4305.8 18.4 all-to-all-start.201
  4436.5 18.4 all-to-all-start.207
  4562.9 18.4 all-to-all-start.213
  4693.6 18.4 all-to-all-start.219
  4820.2 18.4 all-to-all-start.225
  4950.7 18.4 all-to-all-start.231
  5077.3 18.4 all-to-all-start.237
  5208.1 18.4 all-to-all-start.243
  5334.5 18.4 all-to-all-start.249
  5465.2 18.4 all-to-all-start.255
  5591.8 18.4 all-to-all-start.261
  5722.3 18.4 all-to-all-start.267
  5848.9 18.4 all-to-all-start.273
  5975.6 18.4 all-to-all-start.279
  (460 other events, 6978.8 us)
where the time goes:
time: 6220 us; the launch traced here: 6180 us
  waiting for transfers between devices  2490 us (40%)
  local copies, waits for them, and re-layouts  1430 us (23%)
  starting transfers between devices  938 us (15%)
  blocking collectives  776 us (12%)
  matrix products  298 us (5%)
  other arithmetic  235 us (4%)
    all_to_all x96, waiting for transfers between devices, to_channels(): return lax.all_to_all(col_full, 'dap', 0, 1, tiled=True)  1140 us
    all_to_all x96, waiting for transfers between devices, to_channels(): col_full = lax.all_to_all(block, 'dap2', 0, 2, tiled=True)  857 us
    all_to_all x46, blocking collectives, from_channels(): row_part = lax.all_to_all(block, 'dap', 1, 0, tiled=True)  776 us
    all_to_all x48, waiting for transfers between devices, from_channels(): return lax.all_to_all(row_part, 'dap2', 2, 0, tiled=True)  476 us
    all_to_all x192, local copies, waits for them, and re-layouts, to_channels(): col_full = lax.all_to_all(block, 'dap2', 0, 2, tiled=True)  440 us
    all_to_all x96, starting transfers between devices, to_channels(): return lax.all_to_all(col_full, 'dap', 0, 1, tiled=True)  372 us
    all_to_all x96, starting transfers between devices, to_channels(): col_full = lax.all_to_all(block, 'dap2', 0, 2, tiled=True)  357 us
    all_to_all x96, local copies, waits for them, and re-layouts, from_channels(): row_part = lax.all_to_all(block, 'dap', 1, 0, tiled=True)  246 us
  transfers between devices with their start and end apart: 242, of which 242 were waited for; matrix products, arithmetic and copies ran while one was open for 7% of the time, Pallas kernels for 0%

commit v1 on v0

v1 whole, which is shorter than its diff:
```python
import jax
import jax.numpy as jnp
from jax import lax
from jax.experimental import pallas as pl
from jax.experimental.pallas import tpu as pltpu
from jax.sharding import PartitionSpec as P

EPS = 1e-5
F32 = jnp.float32
BF16 = jnp.bfloat16
NT = (((1,), (1,)), ((), ()))
TN = (((0,), (0,)), ((), ()))
MESH = pl.DeviceIdType.MESH


def kernel_body(n_up, z_in, mask_ref, wp_hbm, wgo_hbm, par_hbm, out_ref,
                z, xk, wk, wgo, wps, wgs, par, ab_send, ab_recv, t_send, t_recv,
                ab_ss, ab_rs, t_ss, t_rs, loc_ab, loc_t, psem):
    yy = lax.axis_index("dap2")
    dd = lax.axis_index("dap")
    xx = dd // 2
    cc = dd % 2
    me = dd * 2 + yy

    def peer(s):
        o = 7 - s
        py = (yy + (o // 2) % 2) % 2
        px = (xx + o % 2) % 2
        pc = (cc + o // 4) % 2
        return px * 2 + pc, py

    barrier = pltpu.get_barrier_semaphore()
    for s in range(7):
        pd, py = peer(s)
        pl.semaphore_signal(barrier, inc=1, device_id={"dap2": py, "dap": pd}, device_id_type=MESH)
    pl.semaphore_wait(barrier, 7)

    def ab_copy(h, s):
        pd, py = peer(s)
        return pltpu.make_async_remote_copy(
            src_ref=ab_send.at[h, s],
            dst_ref=ab_recv.at[:, pl.ds(h * 4, 4), pl.ds(dd * 64, 64), pl.ds(yy * 128, 128)],
            send_sem=ab_ss.at[h, s], recv_sem=ab_rs.at[h, s],
            device_id={"dap2": py, "dap": pd}, device_id_type=MESH)

    def ab_local(h):
        return pltpu.make_async_copy(
            ab_send.at[h, 7],
            ab_recv.at[:, pl.ds(h * 4, 4), pl.ds(dd * 64, 64), pl.ds(yy * 128, 128)],
            loc_ab.at[h])

    def t_copy(h, s):
        pd, py = peer(s)
        return pltpu.make_async_remote_copy(
            src_ref=t_send.at[pl.ds(h * 4, 4), pl.ds(pd * 64, 64), pl.ds(py * 128, 128)],
            dst_ref=t_recv.at[pl.ds(me * 8 + h * 4, 4)],
            send_sem=t_ss.at[h, s], recv_sem=t_rs.at[h, s],
            device_id={"dap2": py, "dap": pd}, device_id_type=MESH)

    def t_local(h):
        return pltpu.make_async_copy(
            t_send.at[pl.ds(h * 4, 4), pl.ds(dd * 64, 64), pl.ds(yy * 128, 128)],
            t_recv.at[pl.ds(me * 8 + h * 4, 4)], loc_t.at[h])

    def fetch(u, slot):
        return (pltpu.make_async_copy(wp_hbm.at[u], wps.at[slot], psem.at[slot, 0]),
                pltpu.make_async_copy(wgo_hbm.at[u], wgs.at[slot], psem.at[slot, 1]),
                pltpu.make_async_copy(par_hbm.at[u], par.at[slot], psem.at[slot, 2]))

    delta = (lax.broadcasted_iota(jnp.int32, (8, 512), 0)
             == lax.broadcasted_iota(jnp.int32, (8, 512), 1) % 8).astype(F32)

    def build(src, slot, n, dst):
        def body(k, carry):
            w = src[slot, pl.ds(k * 8, 8)]
            dst[pl.ds(k * 64, 64), :] = (w * delta[None]).reshape(64, 512).astype(BF16)
            return carry
        lax.fori_loop(0, n // 8, body, 0)

    def norm(v, slot, row):
        mean = jnp.sum(v, axis=0) * (1.0 / 64)
        cen = v - mean[None]
        var = jnp.sum(cen * cen, axis=0) * (1.0 / 64)
        rs = lax.rsqrt(var + EPS)
        out = cen * rs[None] * par[slot, row] + par[slot, row + 1]
        return out.reshape(512, 128).astype(BF16)

    for cp in fetch(0, 0):
        cp.start()

    def load_z(r, carry):
        z[:, pl.ds(r * 16, 16), :] = z_in[:, pl.ds(r * 16, 16), :].astype(F32)
        return carry
    lax.fori_loop(0, 4, load_z, 0)
    for cp in fetch(0, 0):
        cp.wait()
    build(wps, 0, 256, wk)

    def update(u, slot):
        nxt = fetch(jnp.minimum(u + 1, n_up - 1), 1 - slot)
        for cp in nxt:
            cp.start()

        def ln_in(r, carry):
            for half in range(2):
                v = z[:, pl.ds(r * 16 + half * 8, 8), :]
                xk[r, :, half * 128:(half + 1) * 128] = norm(v, slot, 0)
            return carry
        lax.fori_loop(0, 4, ln_in, 0)

        for h in range(2):
            def proj(s, carry):
                pd, py = peer(s)
                row = pl.multiple_of(((pd * 2 + py) * 2 + h) * 128, 128)

                def tile(r, carry2):
                    q = jnp.dot(wk[pl.ds(row, 128), :], xk[r], preferred_element_type=F32)
                    q = q.reshape(4, 4, 8, 256)
                    m = mask_ref[r][None]
                    for n in range(2):
                        v = (jnp.tanh(q[2 * n + 1]) + 1.0) * (q[2 * n] * m)
                        v = jnp.concatenate([v[:, :, :128], v[:, :, 128:]], axis=1)
                        ab_send[h, s, n, :, pl.ds(r * 16, 16), :] = v.astype(BF16)
                    return carry2
                lax.fori_loop(0, 4, tile, 0)

                @pl.when(s < 7)
                def _():
                    ab_copy(h, s).start()
                return carry
            lax.fori_loop(0, 8, proj, 0)
            ab_local(h).start()

        for cp in nxt:
            cp.wait()
        build(wps, 1 - slot, 256, wk)
        build(wgs, slot, 128, wgo)

        for h in range(2):
            ab_local(h).wait()
            lax.fori_loop(0, 7, lambda s, c: (ab_copy(h, s).wait_recv(), c)[1], 0)

            def tri(c, carry):
                av = ab_recv[0, h * 4 + c]
                bv = ab_recv[1, h * 4 + c]
                tv = lax.dot_general(av, bv, NT if slot == 0 else TN, preferred_element_type=F32)
                t_send[h * 4 + c] = tv.astype(BF16)
                return carry
            lax.fori_loop(0, 4, tri, 0)
            lax.fori_loop(0, 7, lambda s, c: (t_copy(h, s).start(), c)[1], 0)
            t_local(h).start()
        for h in range(2):
            lax.fori_loop(0, 7, lambda s, c: (ab_copy(h, s).wait_send(), c)[1], 0)
        for h in range(2):
            t_local(h).wait()
            lax.fori_loop(0, 7, lambda s, c: (t_copy(h, s).wait_recv(), c)[1], 0)

        def finish(r, carry):
            tv = t_recv[:, pl.ds(r * 16, 16), :].astype(F32)
            yk = jnp.concatenate([norm(tv[:, :8], slot, 2), norm(tv[:, 8:], slot, 2)], axis=1)
            for k in range(4):
                upd = jnp.dot(wgo[pl.ds(512 + k * 128, 128), :], yk, preferred_element_type=F32)
                gate = jnp.dot(wgo[pl.ds(k * 128, 128), :], xk[r], preferred_element_type=F32)
                inc = ((jnp.tanh(gate) + 1.0) * upd).reshape(16, 8, 256)
                for half in range(2):
                    zv = z[pl.ds(k * 16, 16), pl.ds(r * 16 + half * 8, 8), :]
                    zn = zv + inc[:, :, half * 128:(half + 1) * 128]
                    z[pl.ds(k * 16, 16), pl.ds(r * 16 + half * 8, 8), :] = zn.astype(BF16).astype(F32)
            return carry
        lax.fori_loop(0, 4, finish, 0)
        for h in range(2):
            lax.fori_loop(0, 7, lambda s, c: (t_copy(h, s).wait_send(), c)[1], 0)

    def block(l, carry):
        update(2 * l, 0)
        update(2 * l + 1, 1)
        return carry
    lax.fori_loop(0, n_up // 2, block, 0)

    def store_z(r, carry):
        out_ref[:, pl.ds(r * 16, 16), :] = z[:, pl.ds(r * 16, 16), :].astype(BF16)
        return carry
    lax.fori_loop(0, 4, store_z, 0)


def stack(pair_act, pair_mask, in_gamma, in_beta, w_proj, w_gate, out_gamma, out_beta, w_out):
    n_up = 48
    zc = jnp.transpose(pair_act, (2, 0, 1))
    mask = pair_mask.astype(F32).reshape(4, 2, 8, 128).transpose(0, 2, 1, 3).reshape(4, 8, 256)
    wp = (w_proj.astype(F32) * 0.5).reshape(n_up, 64, 4, 8, 2, 4).transpose(0, 3, 4, 2, 5, 1).reshape(n_up, 256, 64)
    wg = (w_gate.astype(F32) * 0.5).reshape(n_up, 64, 64).transpose(0, 2, 1)
    wo = (w_out.astype(F32) * 0.5).reshape(n_up, 64, 64).transpose(0, 2, 1)
    wp = jnp.repeat(wp, 8, axis=-1)[:, :, None, :]
    wgo = jnp.repeat(jnp.concatenate([wg, wo], axis=1), 8, axis=-1)[:, :, None, :]
    par = jnp.stack([in_gamma, in_beta, out_gamma, out_beta], axis=2).reshape(n_up, 4, 64, 1, 1)
    par = jnp.broadcast_to(par, (n_up, 4, 64, 1, 128))
    vm = pl.BlockSpec(memory_space=pltpu.VMEM)
    hb = pl.BlockSpec(memory_space=pl.ANY)
    dma = pltpu.SemaphoreType.DMA
    out = pl.pallas_call(
        lambda *refs: kernel_body(n_up, *refs),
        out_shape=jax.ShapeDtypeStruct((64, 64, 128), BF16),
        in_specs=[vm, vm, hb, hb, hb],
        out_specs=vm,
        scratch_shapes=[
            pltpu.VMEM((64, 64, 128), F32),
            pltpu.VMEM((4, 512, 256), BF16),
            pltpu.VMEM((2048, 512), BF16),
            pltpu.VMEM((1024, 512), BF16),
            pltpu.VMEM((2, 256, 1, 512), F32),
            pltpu.VMEM((2, 128, 1, 512), F32),
            pltpu.VMEM((2, 4, 64, 1, 128), F32),
            pltpu.VMEM((2, 8, 2, 4, 64, 128), BF16),
            pltpu.VMEM((2, 8, 256, 256), BF16),
            pltpu.VMEM((8, 256, 256), BF16),
            pltpu.VMEM((64, 64, 128), BF16),
            dma((2, 7)), dma((2, 7)), dma((2, 7)), dma((2, 7)),
            dma((2,)), dma((2,)), dma((2, 3)),
        ],
        compiler_params=pltpu.CompilerParams(
            collective_id=0, has_side_effects=True, vmem_limit_bytes=64000000),
        name="tri_stack",
    )(zc, mask, wp, wgo, par)
    return jnp.transpose(out, (1, 2, 0))


def solution(mesh):
    pair = P(('data', 'dap'), 'dap2', None)
    return jax.shard_map(stack, mesh=mesh, in_specs=(pair, P(('data', 'dap'), 'dap2')) + (P(),) * 7,
                         out_specs=pair, check_vma=False)
```

time: 6220 us -> 2090 us (0.34)
  waiting for transfers between devices: 2490 us -> 0 us
  Pallas kernels: 0 us -> 1950 us
  local copies, waits for them, and re-layouts: 1430 us -> 129 us
  starting transfers between devices: 938 us -> 0 us
  blocking collectives: 776 us -> 0 us
  matrix products: 298 us -> 0 us
  other arithmetic: 235 us -> 2.3 us
    all_to_all x242 -> x0, waiting for transfers between devices: 2490 us -> none  [the longest x96 1140 us: to_channels(): return lax.all_to_all(col_full, 'dap', 0, 1, tiled=True)]
    pallas_call x0 -> x1, Pallas kernels: none -> 1950 us  [stack(): pl.pallas_call(lambda *refs: kernel_body(n_up, *refs), out_shape=jax.Shap...]
    all_to_all x242 -> x0, starting transfers between devices: 938 us -> none  [the longest x96 372 us: to_channels(): return lax.all_to_all(col_full, 'dap', 0, 1, tiled=True)]
    all_to_all x432 -> x0, local copies, waits for them, and re-layouts: 851 us -> none  [the longest x192 440 us: to_channels(): col_full = lax.all_to_all(block, 'dap2', 0, 2, tiled=True)]
    all_to_all x46 -> x0, blocking collectives: 776 us -> none  [from_channels(): row_part = lax.all_to_all(block, 'dap', 1, 0, tiled=True)]
    convert_element_type x240 -> x0, local copies, waits for them, and re-layouts: 324 us -> none  [the longest x48 82.2 us: project_local(): (mask_f * jax.nn.sigmoid(projected[3]) * projected[2]).astype(jnp.bfloat16)]
    dot_general x192 -> x0, matrix products: 298 us -> none  [the longest x48 127 us: project_local(): jnp.einsum('ijd,de->ije', normed, w_gate, preferred_element_type=jnp.floa...]
    unnamed x628 -> x18, local copies, waits for them, and re-layouts: 211 us -> 4.74 us
  transfers between devices with their start and end apart: 242 -> 0, of which waited for: 242 -> 0; matrix products, arithmetic and copies ran while one was open for 7% -> 0% of each run, Pallas kernels for 0% -> 0%
where the time goes in v1:
time: 2090 us; the launch traced here: 2080 us
  Pallas kernels  1950 us (93%)
  local copies, waits for them, and re-layouts  129 us (6%)
    pallas_call x1, Pallas kernels, stack(): pl.pallas_call(lambda *refs: kernel_body(n_up, *refs), out_shape=jax.Shap...  1950 us
    another operation x2, local copies, waits for them, and re-layouts, stack(): wp = jnp.repeat(wp, 8, axis=-1)[:, :, None, :]  61.8 us

profile of v1, /device:TPU:0, one launch (start us, length us, event | category | flops | bytes accessed | tf_op | source)
XLA Modules:
  0.0 2082.8 jit_solution(17277481473046730635)
XLA Ops:
  0.0 3.1 copy.18
  3.1 0.7 convert_multiply_fusion
  3.8 6.3 copy.19
  10.1 5.2 copy.20
  15.3 8.6 broadcast_bitcast_fusion
  23.9 0.0 copy-start.1
  23.9 0.0 copy-start.2
  23.9 53.2 %copy.25.refs_2_ = f32[48,256,1,512]{3,2,1,0:T(1,128)} copy(f32[48,256,1,512]{1,3,0,2:T(8,128)} %broadcast_bitcast_fusion) | data formatting | bytes 50331648 | tf_op jit(solution)/shard_map/broadcast_in_dim;reshape | solution.py:193
  77.1 0.0 copy-done.1
  77.1 0.2 convert_multiply_fusion.1
  77.3 0.0 copy-done.2
  77.3 0.2 convert_multiply_fusion.2
  77.5 0.5 pad_maximum_fusion
  78.0 5.4 broadcast_bitcast_fusion.1
  83.4 0.0 copy-start.4
  83.4 0.0 copy-start.5
  83.4 0.0 copy-start.6
  83.4 0.0 copy-start.7
  83.4 27.2 %copy.26.refs_3_ = f32[48,128,1,512]{3,2,1,0:T(1,128)} copy(f32[48,128,1,512]{1,3,0,2:T(8,128)} %broadcast_bitcast_fusion.1) | data formatting | bytes 25165824 | tf_op jit(solution)/shard_map/broadcast_in_dim;reshape | solution.py:194
  110.6 0.0 copy-done.4
  110.6 0.0 copy-done.5
  110.6 0.0 copy-done.6
  110.6 0.0 copy-done.7
  110.6 0.1 maximum_bitcast_fusion
  110.7 0.0 copy-start
  110.8 0.0 copy-start.3
  110.8 15.4 broadcast_in_dim.16.refs_4_
  126.2 0.0 copy-done
  126.2 1.6 copy.29
  127.8 0.0 copy-done.3
  127.8 0.6 convert_element_type.12
  128.4 1951.5 %tri_stack.1 = bf16[64,64,128]{2,1,0:T(8,128)(2,1)} custom-call(bf16[64,64,128]{2,1,0:T(8,128)(2,1)} %bitcast.42, f32[4,8,256]{2,1,0:T(8,128)} %bitcast.43, f32[48,256,1,512]{3,2,1,0:T(1,128)} %copy.25.refs_2_, f32[48,128,1,512]{3,2,1,0:T(1,128)} %copy.26.refs_3_, f32[48,4,64,1,128]{4,3,2,1,0:T(1,128)} %broadcast_in_dim.16.refs_4_), custom_call_target="tpu_custom_call" | custom-call | tf_op jit(solution)/shard_map/tri_stack/pallas_call | solution.py:200
  2079.9 2.9 copy.27
Async XLA Ops:
  23.9 53.2 %copy-start.1 = (bf16[24,2,64,64]{3,2,1,0:T(8,128)(2,1)S(1)}, bf16[24,2,64,64]{3,2,1,0:T(8,128)(2,1)}, u32[]{:S(2)}) copy-start(bf16[24,2,64,64]{3,2,1,0:T(8,128)(2,1)} %param.17) | copy-start | bytes 1179652
  23.9 53.4 %copy-start.2 = (bf16[24,2,64,64]{3,2,1,0:T(8,128)(2,1)S(1)}, bf16[24,2,64,64]{3,2,1,0:T(8,128)(2,1)}, u32[]{:S(2)}) copy-start(bf16[24,2,64,64]{3,2,1,0:T(8,128)(2,1)} %param.14) | copy-start | bytes 1179652
  83.4 27.2 %copy-start.4 = (f32[24,2,64]{2,1,0:T(2,128)S(1)}, f32[24,2,64]{2,1,0:T(2,128)}, u32[]{:S(2)}) copy-start(f32[24,2,64]{2,1,0:T(2,128)} %param.16) | copy-start | bytes 36868
  83.4 27.2 %copy-start.5 = (f32[24,2,64]{2,1,0:T(2,128)S(1)}, f32[24,2,64]{2,1,0:T(2,128)}, u32[]{:S(2)}) copy-start(f32[24,2,64]{2,1,0:T(2,128)} %param.15) | copy-start | bytes 36868
  83.4 27.2 %copy-start.6 = (f32[24,2,64]{2,1,0:T(2,128)S(1)}, f32[24,2,64]{2,1,0:T(2,128)}, u32[]{:S(2)}) copy-start(f32[24,2,64]{2,1,0:T(2,128)} %param.12) | copy-start | bytes 36868
  83.4 27.2 %copy-start.7 = (f32[24,2,64]{2,1,0:T(2,128)S(1)}, f32[24,2,64]{2,1,0:T(2,128)}, u32[]{:S(2)}) copy-start(f32[24,2,64]{2,1,0:T(2,128)} %param.11) | copy-start | bytes 36868
  110.7 15.4 copy-start
  110.8 17.1 copy-start.3

commit v2 on v0

v2 whole, which is shorter than its diff:
```python
import jax
import jax.numpy as jnp
from jax import lax
from jax.experimental import pallas as pl
from jax.experimental.pallas import tpu as pltpu
from jax.sharding import PartitionSpec as P

EPS = 1e-5
F32 = jnp.float32
BF16 = jnp.bfloat16
NT = (((1,), (1,)), ((), ()))
TN = (((0,), (0,)), ((), ()))
MESH = pl.DeviceIdType.MESH
S, Q, H, C, L, W, K = 8, 16, 32, 64, 128, 256, 512
ONE = slice(0, L)
TWO = slice(L, W)
LANES = (ONE, TWO)


def kernel_body(n_up, z_in, mask_ref, w_proj, w_gate, w_out, par_hbm, out_ref,
                z, xk, xm, xoy, po, wk, wgo, wt, rep, par, ao, bo, ai, ar, bi, tp, tpr, tt,
                x_ss, x_rs, b_ss, b_rs, p_ss, p_rs, a_ss, a_rs, t_ss, t_rs, psem):
    yy = lax.axis_index("dap2")
    dd = lax.axis_index("dap")
    xx = dd // 2
    cc = dd % 2
    dx = 2 * (1 - xx) + cc
    ds = 2 * xx + 1 - cc
    own = 2 * yy
    oth = 2 * (1 - yy)
    to_y = {"dap2": 1 - yy, "dap": dd}
    to_x = {"dap2": yy, "dap": dx}
    to_s = {"dap2": yy, "dap": ds}

    barrier = pltpu.get_barrier_semaphore()
    for dev in (to_y, to_x, to_s):
        pl.semaphore_signal(barrier, inc=1, device_id=dev, device_id_type=MESH)
    pl.semaphore_wait(barrier, 3)

    def remote(src, dst, ss, rs, dev):
        return pltpu.make_async_remote_copy(src_ref=src, dst_ref=dst, send_sem=ss, recv_sem=rs,
                                            device_id=dev, device_id_type=MESH)

    def at(start, size):
        return pl.ds(pl.multiple_of(start, size), size)

    def sub(k, n):
        return slice(k * n, k * n + n)

    def b_copy(kind, idx):
        d = (dx if kind == 2 else dd) * H
        if idx < 3:
            ref = bo.at[:, pl.ds(d + idx % 2 * Q, Q), pl.ds(idx // 2 * L, L)]
        else:
            ref = bo.at[pl.ds((idx - 3) * Q, Q), pl.ds(d + Q, Q), pl.ds(L, L)]
        return remote(ref, ref, b_ss.at[kind, idx], b_rs.at[kind, idx], to_x if kind == 0 else to_s)

    def a_copy(idx):
        if idx < 3:
            where = (slice(None), pl.ds(idx * Q, Q))
        else:
            where = (pl.ds((idx - 3) * Q, Q), pl.ds(3 * Q, Q))
        return remote(ai.at[where], ar.at[where], a_ss.at[idx], a_rs.at[idx], to_y)

    def x_copy(r):
        return remote(xm.at[r], xoy.at[r], x_ss.at[r], x_rs.at[r], to_y)

    def p_copy(i):
        return remote(xm.at[i], po.at[i], p_ss.at[i], p_rs.at[i], to_x)

    def t_copy(ck):
        return remote(tp.at[1 - cc, pl.ds(ck * Q, Q)], tpr.at[pl.ds(ck * Q, Q)],
                      t_ss.at[ck], t_rs.at[ck], to_s)

    def fetch(u, slot):
        return pltpu.make_async_copy(par_hbm.at[u], par.at[slot], psem.at[slot])

    def loop(n, fn, unroll=1):
        def body(i, carry):
            fn(i)
            return carry
        lax.fori_loop(0, n, body, 0, unroll=unroll)

    delta = (lax.broadcasted_iota(jnp.int32, (S, K), 0)
             == lax.broadcasted_iota(jnp.int32, (S, K), 1) % S).astype(F32)
    low = lax.broadcasted_iota(jnp.int32, (1, S, L), 2) < C
    low2 = low[0, :1]
    rep[...] = jnp.where(lax.broadcasted_iota(jnp.int32, (C, K), 0)
                         == lax.broadcasted_iota(jnp.int32, (C, K), 1) // S, 0.5, 0.0).astype(BF16)

    def expand(src8, dst, k):
        w = wt[at(src8, S), :]
        rows = [jnp.broadcast_to(w[i:i + 1], (S, K)) * delta for i in range(S)]
        dst[at(k * C, C), :] = jnp.concatenate(rows, axis=0).astype(BF16)

    def spread(w):
        return lax.dot_general(w, rep[...], TN, preferred_element_type=F32)

    def build_wk(u, slot):
        wt[...] = spread(w_proj[u])

        def body(k):
            group = k // Q * 2 + k // 2 % 2
            expand(group * C + k // 4 % 4 * Q + k % 2 * S, wk.at[slot], k)
        loop(H, body)

    def build_wgo(u):
        wt[:C] = spread(w_gate[u])
        wt[C:L] = spread(w_out[u])
        loop(Q, lambda k: expand(k * S, wgo, k))

    def stats(load):
        tot = jnp.sum(load(0), axis=0)
        for k in range(1, 4):
            tot = tot + jnp.sum(load(k), axis=0)
        mean = tot * (1.0 / C)
        sq = jnp.zeros_like(mean)
        for k in range(4):
            cen = load(k) - mean[None]
            sq = sq + jnp.sum(cen * cen, axis=0)
        return mean, lax.rsqrt(sq * (1.0 / C) + EPS)

    def apply(v, st, slot, row, k):
        mean, rs = st
        return (v - mean[None]) * rs[None] * par[slot, row, sub(k, Q)] + par[slot, row + 1, sub(k, Q)]

    def flat(v):
        return v.reshape(L, L).astype(BF16)

    def ab(slot, which, ck, rhs):
        q = jnp.dot(wk[slot, sub(which * 4 + ck, W), :], rhs, preferred_element_type=F32).reshape(2, Q, S, W)
        v = (jnp.tanh(q[1]) + 1.0) * q[0]
        return jnp.concatenate([v[:, :, ONE], v[:, :, TWO]], axis=1).astype(BF16)

    def z_load(i8):
        return lambda k: z[sub(k, Q), at(i8 * S, S), :]

    def fin(r, slot):
        ys = []
        for half in range(2):
            def load(k):
                return tt[sub(k, Q), pl.ds(r * Q, Q), :].astype(F32)[:, sub(half, S)]
            st = stats(load)
            ys.append(jnp.concatenate([flat(apply(load(k), st, slot, 2, k)) for k in range(4)], axis=0))
        yk = jnp.concatenate(ys, axis=1)
        for k in range(4):
            upd = jnp.dot(wgo[sub(4 + k, L), :], yk, preferred_element_type=F32)
            gate = jnp.dot(wgo[sub(k, L), :], xk[r], preferred_element_type=F32)
            inc = ((jnp.tanh(gate) + 1.0) * upd).reshape(Q, S, W)
            for half in range(2):
                rows = at(r * Q + half * S, S)
                zn = z[sub(k, Q), rows, :] + inc[:, :, LANES[half]]
                z[sub(k, Q), rows, :] = zn.astype(BF16).astype(F32)

    def ln_out(r):
        for half in range(2):
            load = z_load(r * 2 + half)
            st = stats(load)
            m = mask_ref[r * 2 + half]
            for k in range(4):
                v = apply(load(k), st, 0, 0, k)
                xk[r, sub(k, L), LANES[half]] = flat(v)
                xm[r, sub(k, L), LANES[half]] = flat(v * m[None])

    def ln_in(p):
        for half in range(2):
            lds = [z_load(p * 2 + half + 4 * e) for e in range(2)]
            sts = [stats(ld) for ld in lds]
            ms = [mask_ref[p * 2 + half + 4 * e] for e in range(2)]
            for k in range(4):
                vs = []
                for e in range(2):
                    v = apply(lds[e](k), sts[e], 1, 0, k)
                    xk[p + 2 * e, sub(k, L), LANES[half]] = flat(v)
                    vs.append(v * ms[e][None])
                xm[p * 2, sub(k, L), LANES[half]] = flat(jnp.where(low, vs[0], pltpu.roll(vs[1], C, 2)))
                xm[p * 2 + 1, sub(k, L), LANES[half]] = flat(jnp.where(low, pltpu.roll(vs[0], C, 2), vs[1]))

    row0 = dd * H

    def b_own(rr):
        for ck in range(4):
            bo[sub(ck, Q), at(row0 + rr * Q, Q), ONE] = ab(0, 1, ck, xm[own + rr])
        b_copy(0, rr).start()
        b_copy(1, rr).start()

    def begin_out(pre, go):
        def rows(r):
            pre(r)
            ln_out(r)
        rows(own)
        go(lambda: b_own(0))
        for e in range(2):
            rows(oth + e)
            go(lambda: x_copy(oth + e).start())
        rows(own + 1)

        def rest():
            x_copy(own).start()
            x_copy(own + 1).start()
            b_own(1)
        go(rest)

    def a_own(p):
        for ck in range(4):
            ai[sub(ck, Q), sub(p, Q), :] = ab(1, 0, ck, xm[p * 2 + xx])
        a_copy(p).start()

    def begin_in(pre):
        for p in range(2):
            pre(p)
            pre(p + 2)
            ln_in(p)
            p_copy(p * 2 + 1 - xx).start()
            a_own(p)
        for p in range(2):
            p_copy(p * 2 + xx).start()

    def outgoing(u):
        nxt = fetch(jnp.minimum(u + 1, n_up - 1), 1)
        nxt.start()

        def ao_rows(r, src, lanes):
            for ck in range(4):
                ao[sub(ck, Q), at(r * Q, Q), lanes] = ab(0, 0, ck, src[r])
        loop(4, lambda r: ao_rows(r, xm, ONE))
        b_copy(0, 0).wait_recv()
        b_copy(2, 0).start()
        x_copy(own).wait_recv()
        for ck in range(4):
            bo[sub(ck, Q), at(row0, Q), TWO] = ab(0, 1, ck, xoy[own])
        b_copy(0, 2).start()
        b_copy(1, 2).start()
        ao_rows(own, xoy, TWO)
        b_copy(0, 1).wait_recv()
        b_copy(2, 1).start()
        x_copy(own + 1).wait_recv()
        for ck in range(4):
            bo[sub(ck, Q), at(row0 + Q, Q), TWO] = ab(0, 1, ck, xoy[own + 1])
            b_copy(0, 3 + ck).start()
            b_copy(1, 3 + ck).start()
        ao_rows(own + 1, xoy, TWO)
        build_wgo(u)
        b_copy(0, 2).wait_recv()
        b_copy(2, 2).start()
        nxt.wait()
        build_wk(jnp.minimum(u + 1, n_up - 1), 1)
        for e in range(2):
            x_copy(oth + e).wait_recv()
            ao_rows(oth + e, xoy, TWO)
        for idx in range(3):
            b_copy(1, idx).wait_recv()
            b_copy(2, idx).wait_recv()
        for r in range(4):
            x_copy(r).wait_send()

        def relay(ck):
            b_copy(0, 3 + ck).wait_recv()
            b_copy(2, 3 + ck).start()
        relay(0)
        for ck in range(4):
            if ck < 3:
                relay(ck + 1)
            b_copy(1, 3 + ck).wait_recv()
            b_copy(2, 3 + ck).wait_recv()

            def tri(c):
                ch = ck * Q + c
                tt[ch] = lax.dot_general(ao[ch], bo[ch], NT, preferred_element_type=F32).astype(BF16)
            loop(Q, tri, Q)
        for kind in range(3):
            for idx in range(7):
                b_copy(kind, idx).wait_send()
        begin_in(lambda r: fin(r, 0))

    def incoming(u, last):
        nxt = fetch(jnp.minimum(u + 1, n_up - 1), 0)
        nxt.start()

        def b_do(src, kset, p, hl):
            for ck in range(4):
                bi[sub(ck, Q), at(kset * H + p * Q, Q), at(hl * L, L)] = ab(1, 1, ck, src[p * 2 + hl])
        loop(2, lambda p: b_do(xm, 0, p, 0))
        loop(2, lambda p: b_do(xm, 0, p, 1))
        for p in range(2):
            p_copy(p * 2 + xx).wait_recv()
            for ck in range(4):
                ai[sub(ck, Q), sub(2 + p, Q), :] = ab(1, 0, ck, po[p * 2 + xx])
                if p == 1:
                    a_copy(3 + ck).start()
            if p == 0:
                a_copy(2).start()
                build_wgo(u)
        loop(2, lambda p: b_do(po, 1, p, xx))
        nxt.wait()
        build_wk(jnp.minimum(u + 1, n_up - 1), 0)

        def late(p):
            p_copy(p * 2 + 1 - xx).wait_recv()
            b_do(po, 1, p, 1 - xx)
        loop(2, late)
        for i in range(4):
            p_copy(i).wait_send()
        for idx in range(3):
            a_copy(idx).wait_recv()

        def add(ck):
            t_copy(ck).wait_recv()
            tt[sub(ck, Q)] = (tp[cc, sub(ck, Q)] + tpr[sub(ck, Q)]).astype(BF16)
        for ck in range(4):
            a_copy(3 + ck).wait_recv()

            def tri(c):
                ch = ck * Q + c
                lhs = jnp.concatenate([ai[ch], ar[ch]], axis=1)
                o = lax.dot_general(lhs, bi[ch], TN, preferred_element_type=F32)
                for e in range(2):
                    top, bot = o[sub(2 * e, C)], o[sub(2 * e + 1, C)]
                    res = (jnp.where(low2, top[:, ONE], bot[:, TWO])
                           + pltpu.roll(jnp.where(low2, top[:, TWO], bot[:, ONE]), C, 1))
                    yo = yy if e == 0 else 1 - yy
                    for h in range(2):
                        tp[h, ch, at(yo * H, H), :] = res[sub(h, H)]
            loop(Q, tri, Q)
            t_copy(ck).start()
            if ck:
                add(ck - 1)
        add(3)

        def go(fn):
            pl.when(jnp.logical_not(last))(fn)
        begin_out(lambda r: fin(r, 1), go)
        for idx in range(7):
            a_copy(idx).wait_send()
        for ck in range(4):
            t_copy(ck).wait_send()

    fetch(0, 0).start()

    def load_z(r):
        z[:, pl.ds(r * Q, Q), :] = z_in[:, pl.ds(r * Q, Q), :].astype(F32)
    loop(4, load_z)
    build_wk(0, 0)
    fetch(0, 0).wait()
    begin_out(lambda r: None, lambda fn: fn())

    def block(l):
        outgoing(2 * l)
        incoming(2 * l + 1, l == n_up // 2 - 1)
    loop(n_up // 2, block)

    def store_z(r):
        out_ref[:, pl.ds(r * Q, Q), :] = z[:, pl.ds(r * Q, Q), :].astype(BF16)
    loop(4, store_z)


def swap_in(v):
    s = v.shape
    v = lax.all_to_all(v.reshape((C, 2, 2, H) + s[2:]), 'dap2', 2, 1, tiled=True)
    return v.reshape(s)


def swap_out(v):
    s = v.shape
    v = lax.all_to_all(v.reshape((C, 4, 1, H) + s[2:]), 'dap2', 1, 2, tiled=True)
    return v.reshape(s)


def stack(pair_act, pair_mask, in_gamma, in_beta, w_proj, w_gate, out_gamma, out_beta, w_out):
    n_up = w_proj.shape[0] * 2
    zc = jnp.transpose(swap_in(pair_act), (2, 0, 1))
    mask = swap_in(pair_mask).astype(F32).reshape(S, S, L)
    par = jnp.stack([in_gamma, in_beta, out_gamma, out_beta], axis=2).reshape(n_up, 4, C, 1, 1)
    par = jnp.broadcast_to(par, (n_up, 4, C, 1, L))
    vm = pl.BlockSpec(memory_space=pltpu.VMEM)
    dma = pltpu.SemaphoreType.DMA

    def buf(*shape, dtype=BF16):
        return pltpu.VMEM(shape, dtype)
    out = pl.pallas_call(
        lambda *refs: kernel_body(n_up, *refs),
        out_shape=jax.ShapeDtypeStruct((C, C, L), BF16),
        in_specs=[vm] * 5 + [pl.BlockSpec(memory_space=pl.ANY)],
        out_specs=vm,
        scratch_shapes=[
            buf(C, C, L, dtype=F32), buf(4, K, W), buf(4, K, W), buf(4, K, W), buf(4, K, W),
            buf(2, 4 * K, K), buf(2 * K, K), buf(W, K, dtype=F32), buf(C, K), buf(2, 4, C, 1, L, dtype=F32),
            buf(C, C, W), buf(C, L, W), buf(C, C, L), buf(C, C, L), buf(C, C, W),
            buf(2, C, C, L, dtype=F32), buf(C, C, L, dtype=F32), buf(C, C, L),
            dma((4,)), dma((4,)), dma((3, 7)), dma((3, 7)), dma((4,)), dma((4,)),
            dma((7,)), dma((7,)), dma((4,)), dma((4,)), dma((2,)),
        ],
        compiler_params=pltpu.CompilerParams(
            collective_id=0, has_side_effects=True, vmem_limit_bytes=64000000),
        name="tri_stack",
    )(zc, mask, w_proj.reshape(n_up, C, W), w_gate.reshape(n_up, C, C), w_out.reshape(n_up, C, C), par)
    return swap_out(jnp.transpose(out, (1, 2, 0)))


def solution(mesh):
    pair = P(('data', 'dap'), 'dap2', None)
    return jax.shard_map(stack, mesh=mesh, in_specs=(pair, P(('data', 'dap'), 'dap2')) + (P(),) * 7,
                         out_specs=pair, check_vma=False)
```

time: 6220 us -> 1570 us (0.25)
  waiting for transfers between devices: 2490 us -> 11.6 us
  Pallas kernels: 0 us -> 1490 us
  local copies, waits for them, and re-layouts: 1430 us -> 43.5 us
  starting transfers between devices: 938 us -> 8.22 us
  blocking collectives: 776 us -> 15.9 us
  matrix products: 298 us -> 0 us
  other arithmetic: 235 us -> 0.77 us
    all_to_all x242 -> x2, waiting for transfers between devices: 2490 us -> 11.6 us  [swap_in(): lax.all_to_all(v.reshape((C, 2, 2, H) + s[2:]), 'dap2', 2, 1, tiled=True)]
    pallas_call x0 -> x1, Pallas kernels: none -> 1490 us  [stack(): pl.pallas_call(lambda *refs: kernel_body(n_up, *refs), out_shape=jax.Shap...]
    all_to_all x242 -> x2, starting transfers between devices: 938 us -> 8.22 us  [swap_in(): lax.all_to_all(v.reshape((C, 2, 2, H) + s[2:]), 'dap2', 2, 1, tiled=True)]
    all_to_all x432 -> x4, local copies, waits for them, and re-layouts: 851 us -> 3.4 us  [the longest x1 2.01 us: swap_out(): lax.all_to_all(v.reshape((C, 4, 1, H) + s[2:]), 'dap2', 1, 2, tiled=True)]
    all_to_all x46 -> x1, blocking collectives: 776 us -> 15.9 us  [swap_out(): lax.all_to_all(v.reshape((C, 4, 1, H) + s[2:]), 'dap2', 1, 2, tiled=True)]
    convert_element_type x240 -> x2, local copies, waits for them, and re-layouts: 324 us -> 0.89 us  [stack(): mask = swap_in(pair_mask).astype(F32).reshape(S, S, L)]
    dot_general x192 -> x0, matrix products: 298 us -> none  [the longest x48 127 us: project_local(): jnp.einsum('ijd,de->ije', normed, w_gate, preferred_element_type=jnp.floa...]
    unnamed x628 -> x16, local copies, waits for them, and re-layouts: 211 us -> 12.4 us
  transfers between devices with their start and end apart: 242 -> 2, of which waited for: 242 -> 1; matrix products, arithmetic and copies ran while one was open for 7% -> 1% of each run, Pallas kernels for 0% -> 0%
where the time goes in v2:
time: 1570 us
  Pallas kernels  1490 us (95%)
  local copies, waits for them, and re-layouts  43.5 us (3%)
  blocking collectives  15.9 us (1%)
    pallas_call x1, Pallas kernels, stack(): pl.pallas_call(lambda *refs: kernel_body(n_up, *refs), out_shape=jax.Shap...  1490 us
  transfers between devices with their start and end apart: 2, of which 1 were waited for; matrix products, arithmetic and copies ran while one was open for 1% of the time, Pallas kernels for 0%

profile of v2, /device:TPU:0, one launch (start us, length us, event | category | flops | bytes accessed | tf_op | source)
XLA Modules:
  0.0 1570.2 jit_solution(12781882242058327308)
XLA Ops:
  0.0 0.8 copy.33
  0.9 0.7 reshape.53
  1.6 4.6 all-to-all-start.1
  6.2 2.8 copy.29
  9.0 2.3 copy.48
  11.2 0.0 copy-start
  11.3 0.0 copy-start.1
  11.3 0.0 copy-start.2
  11.3 0.0 copy-start.3
  11.3 2.4 reshape.51
  13.7 0.0 all-to-all-done.1
  13.7 3.6 all-to-all-start
  17.3 0.0 copy-done
  17.3 0.0 copy-done.1
  17.3 0.0 copy-done.2
  17.4 0.0 copy-done.3
  17.4 0.1 maximum_bitcast_fusion
  17.5 0.5 broadcast.1
  18.0 0.6 reduce
  18.6 0.1 reshape.54
  18.8 0.1 copy.35
  18.9 0.8 convert_element_type.16.refs_1_
  19.7 11.6 all-to-all-done
  31.2 1.3 reshape.52
  32.6 0.4 bitcast_bitcast_fusion
  33.0 0.5 copy.31
  33.5 2.3 copy.32
  35.8 15.3 broadcast_in_dim.8.refs_5_
  51.1 1490.1 %tri_stack.1 = bf16[64,64,128]{2,1,0:T(8,128)(2,1)} custom-call(bf16[64,64,128]{2,1,0:T(8,128)(2,1)} %bitcast.58, f32[8,8,128]{2,1,0:T(8,128)} %convert_element_type.16.refs_1_, bf16[48,64,256]{2,1,0:T(8,128)(2,1)} %bitcast.60, bf16[48,64,64]{2,1,0:T(8,128)(2,1)} %bitcast.61, bf16[48,64,64]{2,1,0:T(8,128)(2,1)} %bitcast.62, ...), custom_call_target="tpu_custom_call" | custom-call | tf_op jit(solution)/shard_map/tri_stack/pallas_call | solution.py:380
  1541.2 2.4 copy.40
  1543.7 1.7 copy.47
  1545.4 2.8 reshape.55
  1548.2 15.9 %all_to_all.39 = bf16[2,2,131072]{2,1,0:T(2,128)(2,1)S(1)} all-to-all(bf16[2,2,131072]{2,1,0:T(2,128)(2,1)S(1)} %reshape.55), channel_id=1, replica_groups=mesh['data'=1,'dap2'=2,'dap'=4] {'dap2'}, dimensions={0} | all-to-all | bytes 2097152 | tf_op jit(solution)/shard_map/all_to_all | solution.py:365
  1564.2 1.3 reshape.56
  1565.5 2.0 copy.42
  1567.5 2.7 copy.43
  (2 shorter events, 0.0 us)
Async XLA Ops:
  1.6 12.2 all-to-all-start.1
  11.2 6.1 copy-start
  11.3 6.1 copy-start.1
  11.3 6.1 copy-start.2
  11.3 6.1 copy-start.3
  13.7 17.5 %all-to-all-start = ((bf16[2,2,131072]{2,1,0:T(2,128)(2,1)}), bf16[2,2,131072]{2,1,0:T(2,128)(2,1)S(1)}, u32[]{:S(2)}, u32[]{:S(2)}) async-start(bf16[2,2,131072]{2,1,0:T(2,128)(2,1)} %reshape.51), calls=%async_computation | async-start | bytes 2097152 | tf_op jit(solution)/shard_map/all_to_all | solution.py:359

commit v3 on v2

--- a/solution.py
+++ b/solution.py
@@ -18,7 +18,7 @@
 
 
 def kernel_body(n_up, z_in, mask_ref, w_proj, w_gate, w_out, par_hbm, out_ref,
-                z, xk, xm, xoy, po, wk, wgo, wt, rep, par, ao, bo, ai, ar, bi, tp, tpr, tt,
+                z, xk, xm, xoy, po, wk, wgo, wt, rep, par, ao, bo, ai, ar, bi, at_, tp, tpr, tt, gt, eye,
                 x_ss, x_rs, b_ss, b_rs, p_ss, p_rs, a_ss, a_rs, t_ss, t_rs, psem):
     yy = lax.axis_index("dap2")
     dd = lax.axis_index("dap")
@@ -66,7 +66,11 @@
         return remote(xm.at[r], xoy.at[r], x_ss.at[r], x_rs.at[r], to_y)
 
     def p_copy(i):
-        return remote(xm.at[i], po.at[i], p_ss.at[i], p_rs.at[i], to_x)
+        if i < 4:
+            where = (i // 2 * 2 + 1 - xx, slice(None), pl.ds(i % 2 * L, L))
+        else:
+            where = (i % 2 * 2 + xx,)
+        return remote(xm.at[where], po.at[where], p_ss.at[i], p_rs.at[i], to_x)
 
     def t_copy(ck):
         return remote(tp.at[1 - cc, pl.ds(ck * Q, Q)], tpr.at[pl.ds(ck * Q, Q)],
@@ -84,7 +88,13 @@
     delta = (lax.broadcasted_iota(jnp.int32, (S, K), 0)
              == lax.broadcasted_iota(jnp.int32, (S, K), 1) % S).astype(F32)
     low = lax.broadcasted_iota(jnp.int32, (1, S, L), 2) < C
-    low2 = low[0, :1]
+    low3 = lax.broadcasted_iota(jnp.int32, (C, L), 1) < C
+
+    def pair(v, w):
+        return jnp.concatenate([jnp.where(low3, v, pltpu.roll(w, C, 1)),
+                                jnp.where(low3, pltpu.roll(v, C, 1), w)], axis=0)
+    eye[...] = (lax.broadcasted_iota(jnp.int32, (L, L), 0)
+                == lax.broadcasted_iota(jnp.int32, (L, L), 1)).astype(F32).astype(BF16)
     rep[...] = jnp.where(lax.broadcasted_iota(jnp.int32, (C, K), 0)
                          == lax.broadcasted_iota(jnp.int32, (C, K), 1) // S, 0.5, 0.0).astype(BF16)
 
@@ -108,6 +118,12 @@
         wt[:C] = spread(w_gate[u])
         wt[C:L] = spread(w_out[u])
         loop(Q, lambda k: expand(k * S, wgo, k))
+
+        def gates(r):
+            for k in range(4):
+                gate = jnp.dot(wgo[sub(k, L), :], xk[r], preferred_element_type=F32)
+                gt[r, sub(k, L), :] = jnp.tanh(gate) + 1.0
+        loop(4, gates)
 
     def stats(load):
         tot = jnp.sum(load(0), axis=0)
@@ -145,8 +161,7 @@
         yk = jnp.concatenate(ys, axis=1)
         for k in range(4):
             upd = jnp.dot(wgo[sub(4 + k, L), :], yk, preferred_element_type=F32)
-            gate = jnp.dot(wgo[sub(k, L), :], xk[r], preferred_element_type=F32)
-            inc = ((jnp.tanh(gate) + 1.0) * upd).reshape(Q, S, W)
+            inc = (gt[r, sub(k, L), :] * upd).reshape(Q, S, W)
             for half in range(2):
                 rows = at(r * Q + half * S, S)
                 zn = z[sub(k, Q), rows, :] + inc[:, :, LANES[half]]
@@ -162,19 +177,19 @@
                 xk[r, sub(k, L), LANES[half]] = flat(v)
                 xm[r, sub(k, L), LANES[half]] = flat(v * m[None])
 
-    def ln_in(p):
-        for half in range(2):
-            lds = [z_load(p * 2 + half + 4 * e) for e in range(2)]
-            sts = [stats(ld) for ld in lds]
-            ms = [mask_ref[p * 2 + half + 4 * e] for e in range(2)]
-            for k in range(4):
-                vs = []
-                for e in range(2):
-                    v = apply(lds[e](k), sts[e], 1, 0, k)
-                    xk[p + 2 * e, sub(k, L), LANES[half]] = flat(v)
-                    vs.append(v * ms[e][None])
-                xm[p * 2, sub(k, L), LANES[half]] = flat(jnp.where(low, vs[0], pltpu.roll(vs[1], C, 2)))
-                xm[p * 2 + 1, sub(k, L), LANES[half]] = flat(jnp.where(low, pltpu.roll(vs[0], C, 2), vs[1]))
+    def ln_in(r):
+        vs = []
+        lds = [z_load(r * 2 + e) for e in range(2)]
+        sts = [stats(ld) for ld in lds]
+        for k in range(4):
+            vs = []
+            for e in range(2):
+                v = apply(lds[e](k), sts[e], 1, 0, k)
+                xk[r, sub(k, L), LANES[e]] = flat(v)
+                vs.append(v * mask_ref[r * 2 + e][None])
+            i = r // 2 * 2
+            xm[i, sub(k, L), LANES[r % 2]] = flat(jnp.where(low, vs[0], pltpu.roll(vs[1], C, 2)))
+            xm[i + 1, sub(k, L), LANES[r % 2]] = flat(jnp.where(low, pltpu.roll(vs[0], C, 2), vs[1]))
 
     row0 = dd * H
 
@@ -188,11 +203,12 @@
         def rows(r):
             pre(r)
             ln_out(r)
+        rows(oth)
+        go(lambda: x_copy(oth).start())
         rows(own)
         go(lambda: b_own(0))
-        for e in range(2):
-            rows(oth + e)
-            go(lambda: x_copy(oth + e).start())
+        rows(oth + 1)
+        go(lambda: x_copy(oth + 1).start())
         rows(own + 1)
 
         def rest():
@@ -207,14 +223,14 @@
         a_copy(p).start()
 
     def begin_in(pre):
+        for r in range(4):
+            pre(r)
+            ln_in(r)
+            p_copy(r).start()
+            if r % 2:
+                a_own(r // 2)
         for p in range(2):
-            pre(p)
-            pre(p + 2)
-            ln_in(p)
-            p_copy(p * 2 + 1 - xx).start()
-            a_own(p)
-        for p in range(2):
-            p_copy(p * 2 + xx).start()
+            p_copy(4 + p).start()
 
     def outgoing(u):
         nxt = fetch(jnp.minimum(u + 1, n_up - 1), 1)
@@ -245,21 +261,22 @@
         b_copy(2, 2).start()
         nxt.wait()
         build_wk(jnp.minimum(u + 1, n_up - 1), 1)
-        for e in range(2):
-            x_copy(oth + e).wait_recv()
-            ao_rows(oth + e, xoy, TWO)
+        def relay(ck):
+            b_copy(0, 3 + ck).wait_recv()
+            b_copy(2, 3 + ck).start()
+        x_copy(oth).wait_recv()
+        ao_rows(oth, xoy, TWO)
+        relay(0)
+        relay(1)
+        x_copy(oth + 1).wait_recv()
+        ao_rows(oth + 1, xoy, TWO)
         for idx in range(3):
             b_copy(1, idx).wait_recv()
             b_copy(2, idx).wait_recv()
         for r in range(4):
             x_copy(r).wait_send()
-
-        def relay(ck):
-            b_copy(0, 3 + ck).wait_recv()
-            b_copy(2, 3 + ck).start()
-        relay(0)
-        for ck in range(4):
-            if ck < 3:
+        for ck in range(4):
+            if ck in (1, 2):
                 relay(ck + 1)
             b_copy(1, 3 + ck).wait_recv()
             b_copy(2, 3 + ck).wait_recv()
@@ -283,7 +300,8 @@
         loop(2, lambda p: b_do(xm, 0, p, 0))
         loop(2, lambda p: b_do(xm, 0, p, 1))
         for p in range(2):
-            p_copy(p * 2 + xx).wait_recv()
+            p_copy(2 * p).wait_recv()
+            p_copy(2 * p + 1).wait_recv()
             for ck in range(4):
                 ai[sub(ck, Q), sub(2 + p, Q), :] = ab(1, 0, ck, po[p * 2 + xx])
                 if p == 1:
@@ -296,36 +314,45 @@
         build_wk(jnp.minimum(u + 1, n_up - 1), 0)
 
         def late(p):
-            p_copy(p * 2 + 1 - xx).wait_recv()
+            p_copy(4 + p).wait_recv()
             b_do(po, 1, p, 1 - xx)
-        loop(2, late)
-        for i in range(4):
-            p_copy(i).wait_send()
+        late(0)
         for idx in range(3):
             a_copy(idx).wait_recv()
 
         def add(ck):
             t_copy(ck).wait_recv()
             tt[sub(ck, Q)] = (tp[cc, sub(ck, Q)] + tpr[sub(ck, Q)]).astype(BF16)
-        for ck in range(4):
+        def turn(ck):
             a_copy(3 + ck).wait_recv()
 
+            def one(c):
+                ch = ck * Q + c
+                at_[ch] = lax.dot_general(pair(ai[ch], ar[ch]), eye[...], TN, preferred_element_type=F32).astype(BF16)
+            loop(Q, one, Q)
+
+        def product(ck):
             def tri(c):
                 ch = ck * Q + c
-                lhs = jnp.concatenate([ai[ch], ar[ch]], axis=1)
-                o = lax.dot_general(lhs, bi[ch], TN, preferred_element_type=F32)
+                o = jnp.dot(at_[ch], pair(bi[ch, :, ONE], bi[ch, :, TWO]), preferred_element_type=F32)
                 for e in range(2):
-                    top, bot = o[sub(2 * e, C)], o[sub(2 * e + 1, C)]
-                    res = (jnp.where(low2, top[:, ONE], bot[:, TWO])
-                           + pltpu.roll(jnp.where(low2, top[:, TWO], bot[:, ONE]), C, 1))
                     yo = yy if e == 0 else 1 - yy
                     for h in range(2):
-                        tp[h, ch, at(yo * H, H), :] = res[sub(h, H)]
+                        tp[h, ch, at(yo * H, H), :] = o[sub(2 * e + h, H)]
             loop(Q, tri, Q)
             t_copy(ck).start()
-            if ck:
-                add(ck - 1)
-        add(3)
+
+        for ck in range(3):
+            turn(ck)
+        late(1)
+        for ck in range(3):
+            product(ck)
+        turn(3)
+        product(3)
+        for i in range(6):
+            p_copy(i).wait_send()
+        for ck in range(4):
+            add(ck)
 
         def go(fn):
             pl.when(jnp.logical_not(last))(fn)
@@ -385,9 +412,9 @@
         scratch_shapes=[
             buf(C, C, L, dtype=F32), buf(4, K, W), buf(4, K, W), buf(4, K, W), buf(4, K, W),
             buf(2, 4 * K, K), buf(2 * K, K), buf(W, K, dtype=F32), buf(C, K), buf(2, 4, C, 1, L, dtype=F32),
-            buf(C, C, W), buf(C, L, W), buf(C, C, L), buf(C, C, L), buf(C, C, W),
-            buf(2, C, C, L, dtype=F32), buf(C, C, L, dtype=F32), buf(C, C, L),
-            dma((4,)), dma((4,)), dma((3, 7)), dma((3, 7)), dma((4,)), dma((4,)),
+            buf(C, C, W), buf(C, L, W), buf(C, C, L), buf(C, C, L), buf(C, C, W), buf(C, L, L),
+            buf(2, C, C, L, dtype=F32), buf(C, C, L, dtype=F32), buf(C, C, L), buf(4, K, W, dtype=F32), buf(L, L),
+            dma((4,)), dma((4,)), dma((3, 7)), dma((3, 7)), dma((6,)), dma((6,)),
             dma((7,)), dma((7,)), dma((4,)), dma((4,)), dma((2,)),
         ],
         compiler_params=pltpu.CompilerParams(

time: 1570 us -> 1500 us (0.955)
  Pallas kernels: 1490 us -> 1420 us
    pallas_call x1, Pallas kernels: 1490 us -> 1420 us  [stack(): pl.pallas_call(lambda *refs: kernel_body(n_up, *refs), out_shape=jax.Shap...]
where the time goes in v3:
time: 1500 us
  Pallas kernels  1420 us (95%)
  local copies, waits for them, and re-layouts  43.5 us (3%)
  blocking collectives  16.7 us (1%)
    pallas_call x1, Pallas kernels, stack(): pl.pallas_call(lambda *refs: kernel_body(n_up, *refs), out_shape=jax.Shap...  1420 us
  transfers between devices with their start and end apart: 2, of which 1 were waited for; matrix products, arithmetic and copies ran while one was open for 1% of the time, Pallas kernels for 0%

profile of v3, /device:TPU:0, one launch (start us, length us, event | category | flops | bytes accessed | tf_op | source)
XLA Modules:
  0.0 1496.6 jit_solution(14070937099719154112)
XLA Ops:
  0.0 0.8 copy.33
  0.9 0.7 reshape.53
  1.6 4.6 all-to-all-start.1
  6.2 2.8 copy.29
  9.0 2.3 copy.48
  11.2 0.0 copy-start
  11.3 0.0 copy-start.1
  11.3 0.0 copy-start.2
  11.3 0.0 copy-start.3
  11.3 2.4 reshape.51
  13.7 0.0 all-to-all-done.1
  13.7 3.6 all-to-all-start
  17.3 0.0 copy-done
  17.3 0.0 copy-done.1
  17.3 0.0 copy-done.2
  17.4 0.0 copy-done.3
  17.4 0.1 maximum_bitcast_fusion
  17.5 0.5 broadcast.1
  18.0 0.6 reduce
  18.6 0.1 reshape.54
  18.8 0.1 copy.35
  18.9 0.8 convert_element_type.16.refs_1_
  19.7 11.6 all-to-all-done
  31.2 1.3 reshape.52
  32.6 0.4 bitcast_bitcast_fusion
  33.0 0.5 copy.31
  33.5 2.3 copy.32
  35.8 15.3 %broadcast_in_dim.8.refs_5_ = f32[48,4,64,1,128]{4,3,2,1,0:T(1,128)} broadcast(f32[48,4,64]{2,1,0:T(4,128)S(1)} %maximum_bitcast_fusion), dimensions={0,1,2} | broadcast | bytes 6340608 | tf_op jit(solution)/shard_map/broadcast_in_dim | solution.py:401
  51.1 1415.6 %tri_stack.1 = bf16[64,64,128]{2,1,0:T(8,128)(2,1)} custom-call(bf16[64,64,128]{2,1,0:T(8,128)(2,1)} %bitcast.58, f32[8,8,128]{2,1,0:T(8,128)} %convert_element_type.16.refs_1_, bf16[48,64,256]{2,1,0:T(8,128)(2,1)} %bitcast.60, bf16[48,64,64]{2,1,0:T(8,128)(2,1)} %bitcast.61, bf16[48,64,64]{2,1,0:T(8,128)(2,1)} %bitcast.62, ...), custom_call_target="tpu_custom_call" | custom-call | tf_op jit(solution)/shard_map/tri_stack/pallas_call | solution.py:407
  1466.8 2.4 copy.40
  1469.2 1.7 copy.47
  1471.0 2.8 reshape.55
  1473.8 16.7 %all_to_all.39 = bf16[2,2,131072]{2,1,0:T(2,128)(2,1)S(1)} all-to-all(bf16[2,2,131072]{2,1,0:T(2,128)(2,1)S(1)} %reshape.55), channel_id=1, replica_groups=mesh['data'=1,'dap2'=2,'dap'=4] {'dap2'}, dimensions={0} | all-to-all | bytes 2097152 | tf_op jit(solution)/shard_map/all_to_all | solution.py:392
  1490.5 1.3 reshape.56
  1491.9 2.0 copy.42
  1493.9 2.7 copy.43
  (2 shorter events, 0.0 us)
Async XLA Ops:
  1.6 12.2 all-to-all-start.1
  11.2 6.1 copy-start
  11.3 6.1 copy-start.1
  11.3 6.1 copy-start.2
  11.3 6.1 copy-start.3
  13.7 17.5 %all-to-all-start = ((bf16[2,2,131072]{2,1,0:T(2,128)(2,1)}), bf16[2,2,131072]{2,1,0:T(2,128)(2,1)S(1)}, u32[]{:S(2)}, u32[]{:S(2)}) async-start(bf16[2,2,131072]{2,1,0:T(2,128)(2,1)} %reshape.51), calls=%async_computation | async-start | bytes 2097152 | tf_op jit(solution)/shard_map/all_to_all | solution.py:386
